TPU v7x, 512 devices: a whole 4x4x16 slice. The times are simulated.
512 devices in a mesh: dp: 64 (over z, y_lo, core), mp: 8 (over x, y_hi).
Axes of the slice: x: 4, y: 4 (y_hi: 2, y_lo: 2; y = y_hi * 2 + y_lo), z: 16, core: 2. Of those that a mesh axis runs over, the one named last changes fastest.
Arguments:
- picture_tower_vectors: bfloat16 [12288, 1152], P('dp'), may hold values from -6 to 6
- caption_tower_vectors: bfloat16 [12288, 1152], P('dp', 'mp'), may hold values from -6 to 6
- picture_standardize_factor: float32 [1152], replicated, may hold values from 0.1 to 1.9
- picture_entry_matrix: bfloat16 [1152, 4304], P(None, 'mp'), may hold values from -0.1875 to 0.1875
- picture_exit_matrix: bfloat16 [4304, 1152], P('mp'), may hold values from -0.09375 to 0.09375
- caption_mapping_matrix: bfloat16 [1152, 1152], P('mp'), may hold values from -1 to 1
- energy_multiplier: float32 [], replicated, may hold values from 4 to 16
- energy_offset_term: float32 [], replicated, may hold values from -2 to -0.5
Outputs:
- grad_image: float32 [12288, 1152], P('dp', 'mp')
- grad_text: float32 [12288, 1152], P('dp', 'mp')
All inputs are finite; a program needn't handle non-finite values.
Results may differ from a plain program's by a relative error of at most 0.0046.
Values may be sent and summed in bfloat16 or wider, within the bound.
No kernel may reach another device: no remote copies, remote signals or barrier semaphores. Data moves between devices by JAX's collectives and lax.ppermute only.
A program may use at most 64 MiB of HBM per device.

v0:
```python
import jax
import jax.numpy as jnp
from jax import lax
from jax.sharding import Mesh
from jax.sharding import PartitionSpec as P

DP = ("dp_0", "dp_1", "dp_2")


def cut_along(array, dim, peers):
    lengths = array.shape
    parts = array.reshape(*lengths[:dim], peers, lengths[dim] // peers, *lengths[dim + 1 :])
    return jnp.moveaxis(parts, dim, 0)


def summed_on_arrival(array, axis, dim):
    peers = lax.axis_size(axis)
    parts = lax.all_to_all(cut_along(array, dim, peers), axis, 0, 0, tiled=True)
    return jnp.sum(parts.astype(jnp.float32), axis=0)


def in_order(parts, dim):
    lengths = list(parts.shape[1:])
    lengths[dim] *= parts.shape[0]
    return jnp.moveaxis(parts, 0, dim).reshape(lengths)


def stacked_from(array, axes, order):
    parts = array[None]
    for k in order:
        parts = lax.all_gather(parts, axes[k], axis=0, tiled=True)
    block = [lax.axis_size(axes[k]) for k in reversed(order)]
    parts = parts.reshape(*block, *array.shape)
    turned = sorted(range(len(order)), key=lambda place: order[len(order) - 1 - place])
    return parts.transpose(*turned, *range(len(order), parts.ndim)).reshape(-1, *array.shape)


def whole_of(array, axes, order, dim):
    return in_order(stacked_from(array, axes, order), dim)


def sum_at_owner(array, axis, dim):
    parts = cut_along(array, dim, lax.axis_size(axis))
    arrived = lax.all_to_all(parts, axis, split_axis=0, concat_axis=0, tiled=True)
    return arrived.sum(axis=0)


def sent_to_all(array, axis):
    copies = jnp.broadcast_to(array, (lax.axis_size(axis), *array.shape))
    return lax.all_to_all(copies, axis, split_axis=0, concat_axis=0, tiled=True)


def collect(array, axis, dim):
    return in_order(sent_to_all(array, axis), dim)


def of_everyone(array, axis):
    return sent_to_all(array, axis).sum(axis=0)


def together(arrays, axis):
    ends = [0]
    for a in arrays:
        ends.append(ends[-1] + a.size)
    so_far = of_everyone(jnp.concatenate([a.ravel() for a in arrays]), axis)
    return tuple((so_far[b:e].reshape(a.shape) for a, b, e in zip(arrays, ends, ends[1:])))


def gelu_tanh(values):
    return jax.nn.gelu(values, approximate=True)


def norm_back(upstream, unit_rows, inverse):
    unit_float = unit_rows.astype(jnp.float32)
    along = jnp.sum(unit_float * upstream, axis=-1, keepdims=True)
    return inverse * (upstream - unit_float * along)


def per_device(
    picture_tower_vectors,
    caption_tower_vectors,
    picture_standardize_factor,
    picture_entry_matrix,
    picture_exit_matrix,
    caption_mapping_matrix,
    energy_multiplier,
    energy_offset_term,
):
    rows_here = picture_tower_vectors.shape[0]
    width = picture_tower_vectors.shape[1]
    head_count = lax.axis_size("mp")
    head_pos = lax.axis_index("mp")
    cycle_size = lax.axis_size(DP)
    cycle_pos = lax.axis_index(DP)
    share = rows_here // head_count
    cols_here = caption_tower_vectors.shape[1]
    image_float = picture_tower_vectors.astype(jnp.float32)
    mean_row = jnp.mean(image_float, axis=-1, keepdims=True)
    variance = jnp.mean((image_float - mean_row) ** 2, axis=-1, keepdims=True)
    inv_std = lax.rsqrt(variance + 1e-06)
    centred = (image_float - mean_row) * inv_std
    normed = (centred * picture_standardize_factor).astype(jnp.bfloat16)
    preact = jnp.dot(normed, picture_entry_matrix, preferred_element_type=jnp.float32)
    hidden = gelu_tanh(preact).astype(jnp.bfloat16)
    partial_out = jnp.dot(hidden, picture_exit_matrix, preferred_element_type=jnp.float32)
    image_out = image_float + lax.psum(partial_out, "mp")
    inv_image = lax.rsqrt(jnp.sum(image_out * image_out, axis=-1, keepdims=True) + 1e-06)
    unit_image = (image_out * inv_image).astype(jnp.bfloat16)
    text_out = summed_on_arrival(
        jnp.dot(
            caption_tower_vectors, caption_mapping_matrix, preferred_element_type=jnp.float32
        ).astype(jnp.bfloat16),
        "mp",
        0,
    )
    inv_text = lax.rsqrt(jnp.sum(text_out * text_out, axis=-1, keepdims=True) + 1e-06)
    unit_text = (text_out * inv_text).astype(jnp.bfloat16)
    image_ids = cycle_pos * rows_here + jnp.arange(rows_here, dtype=jnp.int32)
    piece = whole_of(unit_text, DP, (1, 0, 2), 0)
    count = piece.shape[0]
    whole_pos = jnp.arange(count, dtype=jnp.int32)
    text_ids = whole_pos // share * rows_here + head_pos * share + whole_pos % share
    cosine_matrix = lax.dot_general(
        piece, unit_image, (((1,), (1,)), ((), ())), preferred_element_type=jnp.float32
    )
    couple_energies = energy_multiplier * cosine_matrix + energy_offset_term
    match_polarity = jnp.where(text_ids[:, None] == image_ids[None, :], 1.0, -1.0).astype(
        jnp.float32
    )
    polarity_scaled_energies = (
        energy_multiplier * -match_polarity * jax.nn.sigmoid(-match_polarity * couple_energies)
    ).astype(jnp.bfloat16)
    image_add = lax.dot_general(
        polarity_scaled_energies,
        piece,
        (((0,), (0,)), ((), ())),
        preferred_element_type=jnp.float32,
    )
    text_add = jnp.dot(polarity_scaled_energies, unit_image, preferred_element_type=jnp.float32)
    image_add, text_add = (image_add, text_add)
    text_store = text_add
    image_dir, text_store = (image_add, text_store)
    returned = lax.all_to_all(
        text_store.astype(jnp.bfloat16), DP, split_axis=0, concat_axis=0, tiled=True
    ).astype(text_store.dtype)
    text_dir = jnp.sum(returned.reshape(cycle_size, share, width), axis=0)
    image_share = sum_at_owner(image_dir, "mp", 0)
    first_row = head_pos * share
    unit_share = lax.dynamic_slice_in_dim(unit_image, first_row, share, 0)
    inv_share = lax.dynamic_slice_in_dim(inv_image, first_row, share, 0)
    grad_share = norm_back(image_share, unit_share, inv_share)
    grad_out = collect(grad_share, "mp", 0)
    grad_out_b = grad_out.astype(jnp.bfloat16)
    grad_hidden = lax.dot_general(
        grad_out_b,
        picture_exit_matrix,
        (((1,), (1,)), ((), ())),
        preferred_element_type=jnp.float32,
    )
    unused, pull_back = jax.vjp(gelu_tanh, preact)
    grad_pre = pull_back(grad_hidden)[0].astype(jnp.bfloat16)
    partial_normed = lax.dot_general(
        grad_pre, picture_entry_matrix, (((1,), (1,)), ((), ())), preferred_element_type=jnp.float32
    )
    grad_normed = sum_at_owner(partial_normed, "mp", 1)
    first_col = head_pos * cols_here
    gain_here = lax.dynamic_slice_in_dim(picture_standardize_factor, first_col, cols_here, 0)
    centred_here = lax.dynamic_slice_in_dim(centred, first_col, cols_here, 1)
    grad_out_here = lax.dynamic_slice_in_dim(grad_out, first_col, cols_here, 1)
    scaled = grad_normed * gain_here
    sum_one, sum_two = together(
        (jnp.sum(scaled, axis=-1), jnp.sum(scaled * centred_here, axis=-1)), "mp"
    )
    mean_one = (sum_one / width)[:, None]
    mean_two = (sum_two / width)[:, None]
    grad_image = grad_out_here + inv_std * (scaled - mean_one - centred_here * mean_two)
    grad_text_out = norm_back(text_dir, unit_text, inv_text).astype(jnp.bfloat16)
    grad_text = lax.dot_general(
        collect(grad_text_out, "mp", 0),
        caption_mapping_matrix,
        (((1,), (1,)), ((), ())),
        preferred_element_type=jnp.float32,
    )
    return (grad_image, grad_text)


def solution(mesh):
    split = Mesh(mesh.devices.reshape(16, 2, 2, mesh.shape["mp"]), ("dp_0", "dp_1", "dp_2", "mp"))
    in_specs = (
        P(DP, None),
        P(DP, "mp"),
        P(),
        P(None, "mp"),
        P("mp", None),
        P("mp", None),
        P(),
        P(),
    )
    out_specs = (P(DP, "mp"), P(DP, "mp"))
    return jax.shard_map(
        per_device, mesh=split, in_specs=in_specs, out_specs=out_specs, check_vma=False
    )
```

profile of v0, /device:TPU:8, one launch (start us, length us, event | category | flops | bytes accessed | tf_op | source)
XLA Modules:
  0.0 417.5 jit_solution(5761427556059178533)
XLA Ops:
  8.0 0.0 copy-start
  8.0 0.0 all-gather.3.cloned.1.call-start
  8.1 1.4 convolution_convert_fusion.1
  9.5 0.0 copy-start.1
  9.5 16.4 %all_to_all.40 = bf16[8,24,1152]{2,1,0:T(8,128)(2,1)S(1)} all-to-all(bf16[8,24,1152]{2,1,0:T(8,128)(2,1)S(1)} %bitcast.50), channel_id=1, replica_groups=mesh['dp_0'=16,'dp_1'=2,'dp_2'=2,'mp'=8] {'mp'}, dimensions={0} | all-to-all | bytes 884736 | tf_op jit(solution)/shard_map/all_to_all | solution.py:18
  25.9 0.1 convert_reduce_fusion.2
  26.0 0.1 multiply_reduce_fusion.3
  26.1 0.1 fusion.50
  26.2 4.9 %all_gather.9 = bf16[2,24,1152]{2,1,0:T(8,128)(2,1)} all-gather(bf16[1,24,1152]{2,1,0:T(8,128)(2,1)S(1)} %fusion.50), channel_id=1, replica_groups=mesh['dp_0'=16,'dp_1'=2,'dp_2'=2,'mp'=8] {'dp_1'}, dimensions={0}, use_global_device_ids=true | all-gather | bytes 165888 | tf_op jit(solution)/shard_map/all_gather | solution.py:31
  31.1 0.0 all-gather.3.cloned.1.call-update
  31.2 0.0 all-reduce.2.cloned.1.call-start
  31.2 0.0 copy-done.1
  31.2 0.1 convert_reduce_fusion.1
  31.4 0.3 fusion.9
  31.7 0.0 copy-done.7
  31.7 2.0 fusion.22
  33.7 0.0 copy-done
  33.7 0.0 copy-start.6
  33.7 1.5 fusion.32
  35.1 0.0 copy-done.6
  35.1 0.0 all-reduce.2.cloned.1.call-update
  35.2 0.0 all-gather.5.cloned.1.call-start
  35.2 69.5 %all-gather.3.cloned.1.call-done = bf16[32,24,1152]{2,1,0:T(8,128)(2,1)} async-done(((bf16[2,24,1152]{2,1,0:T(8,128)(2,1)}), bf16[32,24,1152]{2,1,0:T(8,128)(2,1)}) %all-gather.3.cloned.1.call-update) | async-done | bytes 1769488 | tf_op jit(solution)/shard_map/all_gather | solution.py:31
  104.7 0.0 all-gather.5.cloned.1.call-update
  106.1 33.0 %all-reduce.2.cloned.1.call-done = f32[192,1152]{1,0:T(8,128)} async-done(((f32[192,1152]{1,0:T(8,128)}), f32[192,1152]{1,0:T(8,128)}) %all-reduce.2.cloned.1.call-update) | async-done | bytes 884752 | tf_op jit(solution)/shard_map/psum | solution.py:106
  139.1 1.5 multiply_reduce_fusion
  140.6 0.3 fusion.7
  140.9 0.0 all-gather.5.cloned.1.call-done
  140.9 2.4 copy.22
  143.3 0.0 copy-done.5
  143.4 2.5 fusion.6
  145.9 1.9 fusion.74
  147.8 3.8 all-to-all-start.1
  151.6 0.1 dynamic-slice.3
  151.6 11.3 %all-to-all-done.1 = f32[8,24,1152]{2,1,0:T(8,128)S(1)} async-done(((f32[8,24,1152]{2,1,0:T(8,128)}), f32[8,24,1152]{2,1,0:T(8,128)S(1)}, u32[]{:S(2)}, u32[]{:S(2)}) %all-to-all-start.1) | async-done | bytes 884768 | tf_op jit(solution)/shard_map/all_to_all | solution.py:44
  162.9 0.9 fusion.43
  163.9 0.9 fusion.45
  164.8 0.1 broadcast_in_dim.36
  164.9 15.6 %all_to_all.41 = f32[8,24,1152]{2,1,0:T(8,128)S(1)} all-to-all(f32[8,24,1152]{2,1,0:T(8,128)S(1)} %broadcast_in_dim.36), channel_id=1, replica_groups=mesh['dp_0'=16,'dp_1'=2,'dp_2'=2,'mp'=8] {'mp'}, dimensions={0} | all-to-all | bytes 1769472 | tf_op jit(solution)/shard_map/all_to_all | solution.py:50
  180.5 4.1 fusion.28
  184.6 3.6 all-to-all-start.3
  188.2 0.1 dynamic_slice.15
  188.3 12.4 %all-to-all-done.3 = f32[8,192,144]{1,2,0:T(8,128)S(1)} async-done(((f32[8,192,144]{1,2,0:T(8,128)}), f32[8,192,144]{1,2,0:T(8,128)S(1)}, u32[]{:S(2)}, u32[]{:S(2)}) %all-to-all-start.3) | async-done | bytes 884768 | tf_op jit(solution)/shard_map/all_to_all | solution.py:44
  200.6 0.7 reduce_sum.127
  201.4 1.0 copy.24
  202.4 0.2 multiply_reduce_fusion.2
  202.6 0.1 pad_maximum_fusion
  202.7 0.6 broadcast_in_dim.37
  203.3 4.0 all-to-all-start.4
  207.3 4.7 %convolution_convert_fusion = bf16[1536,1152]{1,0:T(8,128)(2,1)} fusion(bf16[192,1152]{1,0:T(8,128)(2,1)} %copy-done.5, f32[1536,192]{0,1:T(8,128)} %get-tuple-element.19, s32[1536]{0:T(1024)S(1)} %fusion.59, f32[]{:T(128)S(6)} %copy.32, s32[192]{0:T(256)S(1)} %iota_add_fusion), kind=kOutput, calls=%fused_computation | convolution fusion | flops 684195840 | bytes 5167876 | tf_op jit(solution)/shard_map/dot_general | solution.py:139
  212.0 2.9 all-to-all-done.4
  215.0 14.4 %all-to-all-start.5 = ((bf16[64,24,1152]{2,1,0:T(8,128)(2,1)}), bf16[64,24,1152]{2,1,0:T(8,128)(2,1)}, u32[]{:S(2)}, u32[]{:S(2)}) async-start(bf16[64,24,1152]{2,1,0:T(8,128)(2,1)} %bitcast.48), calls=%async_computation.5 | async-start | bytes 7077888 | tf_op jit(solution)/shard_map/all_to_all | solution.py:143
  229.4 162.7 %all-to-all-done.5 = bf16[64,24,1152]{2,1,0:T(8,128)(2,1)} async-done(((bf16[64,24,1152]{2,1,0:T(8,128)(2,1)}), bf16[64,24,1152]{2,1,0:T(8,128)(2,1)}, u32[]{:S(2)}, u32[]{:S(2)}) %all-to-all-start.5) | async-done | bytes 3538976 | tf_op jit(solution)/shard_map/all_to_all | solution.py:143
  392.1 2.5 convert_reduce_fusion
  394.6 0.2 fusion.46
  394.8 0.1 fusion.49
  394.9 0.0 copy-start.3
  394.9 0.8 broadcast_in_dim.40
  395.7 4.3 %all-to-all-start.6 = ((bf16[8,24,1152]{2,1,0:T(8,128)(2,1)}), bf16[8,24,1152]{2,1,0:T(8,128)(2,1)S(1)}, u32[]{:S(2)}, u32[]{:S(2)}) async-start(bf16[8,24,1152]{2,1,0:T(8,128)(2,1)} %broadcast_in_dim.40), calls=%async_computation.6 | async-start | bytes 884736 | tf_op jit(solution)/shard_map/all_to_all | solution.py:50
  400.0 0.1 slice_multiply_fusion.1
  400.0 1.2 multiply_add_fusion
  401.2 0.8 copy.26
  402.0 7.1 %all-to-all-done.6 = bf16[8,24,1152]{2,1,0:T(8,128)(2,1)S(1)} async-done(((bf16[8,24,1152]{2,1,0:T(8,128)(2,1)}), bf16[8,24,1152]{2,1,0:T(8,128)(2,1)S(1)}, u32[]{:S(2)}, u32[]{:S(2)}) %all-to-all-start.6) | async-done | bytes 442400 | tf_op jit(solution)/shard_map/all_to_all | solution.py:50
  409.1 1.0 fusion.75
  (15 shorter events, 0.1 us)
Async XLA Ops:
  8.0 25.7 %copy-start = (bf16[538,1152]{1,0:T(8,128)(2,1)S(1)}, bf16[538,1152]{1,0:T(8,128)(2,1)}, u32[]{:S(2)}) copy-start(bf16[538,1152]{1,0:T(8,128)(2,1)} %param.12) | copy-start | bytes 3718660
  8.0 96.7 %all-gather.3.cloned.1.call-start = ((), (), s32[]{:S(2)}) async-start(), calls=%async_computation.8 | async-start | bytes 1880064 | tf_op jit(solution)/shard_map/all_gather | solution.py:31
  9.5 21.7 %copy-start.1 = (bf16[192,1152]{1,0:T(8,128)(2,1)S(1)}, bf16[192,1152]{1,0:T(8,128)(2,1)}, u32[]{:S(2)}) copy-start(bf16[192,1152]{1,0:T(8,128)(2,1)} %param.8) | copy-start | bytes 1327108
  25.9 5.7 %copy-start.7 = (f32[1152]{0:T(1024)S(1)}, f32[1152]{0:T(1024)}, u32[]{:S(2)}) copy-start(f32[1152]{0:T(1024)} %param.10) | copy-start | bytes 13828
  31.2 107.9 %all-reduce.2.cloned.1.call-start = ((), (), s32[]{:S(2)}) async-start(), calls=%async_computation.7 | async-start | bytes 1769472 | tf_op jit(solution)/shard_map/psum | solution.py:106
  33.7 1.5 copy-start.6
  35.2 105.7 %all-gather.5.cloned.1.call-start = ((), (), s32[]{:S(2)}) async-start(), calls=%async_computation.9 | async-start | bytes 5308416 | tf_op jit(solution)/shard_map/all_gather | solution.py:31
  139.1 1.5 copy-start.2
  140.9 2.5 copy-start.5
  147.8 15.1 %all-to-all-start.1 = ((f32[8,24,1152]{2,1,0:T(8,128)}), f32[8,24,1152]{2,1,0:T(8,128)S(1)}, u32[]{:S(2)}, u32[]{:S(2)}) async-start(f32[8,24,1152]{2,1,0:T(8,128)} %fusion.74), calls=%async_computation.1 | async-start | bytes 1769472 | tf_op jit(solution)/shard_map/all_to_all | solution.py:44
  180.4 4.2 copy-start.4
  184.6 16.0 %all-to-all-start.3 = ((f32[8,192,144]{1,2,0:T(8,128)}), f32[8,192,144]{1,2,0:T(8,128)S(1)}, u32[]{:S(2)}, u32[]{:S(2)}) async-start(f32[8,192,144]{1,2,0:T(8,128)} %bitcast.53), calls=%async_computation.3 | async-start | bytes 2359296 | tf_op jit(solution)/shard_map/all_to_all | solution.py:44
  203.3 11.7 %all-to-all-start.4 = ((f32[8,1,384]{2,1,0:T(1,128)}), f32[8,1,384]{2,1,0:T(1,128)S(1)}, u32[]{:S(2)}, u32[]{:S(2)}) async-start(f32[8,1,384]{2,1,0:T(1,128)} %broadcast_in_dim.37), calls=%async_computation.4 | async-start | bytes 24576 | tf_op jit(solution)/shard_map/all_to_all | solution.py:50
  215.0 177.1 %all-to-all-start.5 = ((bf16[64,24,1152]{2,1,0:T(8,128)(2,1)}), bf16[64,24,1152]{2,1,0:T(8,128)(2,1)}, u32[]{:S(2)}, u32[]{:S(2)}) async-start(bf16[64,24,1152]{2,1,0:T(8,128)(2,1)} %bitcast.48), calls=%async_computation.5 | async-start | bytes 7077888 | tf_op jit(solution)/shard_map/all_to_all | solution.py:143
  394.9 14.2 %copy-start.3 = (bf16[144,1152]{1,0:T(8,128)(2,1)S(1)}, bf16[144,1152]{1,0:T(8,128)(2,1)}, u32[]{:S(2)}) copy-start(bf16[144,1152]{1,0:T(8,128)(2,1)} %param.13) | copy-start | bytes 995332
  395.7 13.4 %all-to-all-start.6 = ((bf16[8,24,1152]{2,1,0:T(8,128)(2,1)}), bf16[8,24,1152]{2,1,0:T(8,128)(2,1)S(1)}, u32[]{:S(2)}, u32[]{:S(2)}) async-start(bf16[8,24,1152]{2,1,0:T(8,128)(2,1)} %broadcast_in_dim.40), calls=%async_computation.6 | async-start | bytes 884736 | tf_op jit(solution)/shard_map/all_to_all | solution.py:50
Sparse Core Ops, SparseCore 0:
  31.3 73.3 all-gather.2
  106.8 20.0 all-gather.4
Sparse Core Ops, SparseCore 1:
  35.3 103.8 all-reduce.1
where the time goes:
time: 419 us; the launch traced here: 418 us
  waiting for transfers between devices  299 us (71%)
  blocking collectives  36.9 us (9%)
  starting transfers between devices  30.1 us (7%)
  matrix products  19.2 us (5%)
  between operations  17 us (4%)
  other arithmetic  9.52 us (2%)
  local copies, waits for them, and re-layouts  5.88 us (1%)
    all_to_all x1, waiting for transfers between devices, per_device(): lax.all_to_all(text_store.astype(jnp.bfloat16), DP, split_axis=0, concat_...  163 us
    all_gather x2, waiting for transfers between devices, stacked_from(): parts = lax.all_gather(parts, axes[k], axis=0, tiled=True)  69.5 us
    psum x1, waiting for transfers between devices, per_device(): image_out = image_float + lax.psum(partial_out, 'mp')  33 us
    all_to_all x2, waiting for transfers between devices, sum_at_owner(): lax.all_to_all(parts, axis, split_axis=0, concat_axis=0, tiled=True)  23.6 us
    all_to_all x1, blocking collectives, summed_on_arrival(): parts = lax.all_to_all(cut_along(array, dim, peers), axis, 0, 0, tiled=True)  16.4 us
    all_to_all x1, blocking collectives, sent_to_all(): return lax.all_to_all(copies, axis, split_axis=0, concat_axis=0, tiled=True)  15.6 us
    all_to_all x1, starting transfers between devices, per_device(): lax.all_to_all(text_store.astype(jnp.bfloat16), DP, split_axis=0, concat_...  14.4 us
    all_to_all x2, waiting for transfers between devices, sent_to_all(): return lax.all_to_all(copies, axis, split_axis=0, concat_axis=0, tiled=True)  10 us
  transfers between devices with their start and end apart: 8, of which 7 were waited for; matrix products, arithmetic and copies ran while one was open for 3% of the time, Pallas kernels for 0%

commit v1 on v0

--- a/solution.py
+++ b/solution.py
@@ -28,7 +28,9 @@
 def stacked_from(array, axes, order):
     parts = array[None]
     for k in order:
-        parts = lax.all_gather(parts, axes[k], axis=0, tiled=True)
+        parts = jnp.concatenate(
+            lax.all_to_all(jnp.stack([parts] * lax.axis_size(axes[k])), axes[k], 0, 0), axis=0
+        )
     block = [lax.axis_size(axes[k]) for k in reversed(order)]
     parts = parts.reshape(*block, *array.shape)
     turned = sorted(range(len(order)), key=lambda place: order[len(order) - 1 - place])

time: 419 us -> 447 us (1.067)
  starting transfers between devices: 30.1 us -> 44.7 us
  blocking collectives: 36.9 us -> 48 us
    all_gather x2 -> x0, waiting for transfers between devices: 69.5 us -> none  [stacked_from(): parts = lax.all_gather(parts, axes[k], axis=0, tiled=True)]
    psum x1, waiting for transfers between devices: 33 us -> 100 us  [per_device(): image_out = image_float + lax.psum(partial_out, 'mp')]
    all_to_all x0 -> x1, starting transfers between devices: none -> 15 us  [stacked_from(): lax.all_to_all(jnp.stack([parts] * lax.axis_size(axes[k])), axes[k], 0, 0)]
    all_to_all x0 -> x2, blocking collectives: none -> 12.9 us  [stacked_from(): lax.all_to_all(jnp.stack([parts] * lax.axis_size(axes[k])), axes[k], 0, 0)]
    all_to_all x2, waiting for transfers between devices: 23.6 us -> 30.3 us  [sum_at_owner(): lax.all_to_all(parts, axis, split_axis=0, concat_axis=0, tiled=True)]
    all_gather x1 -> x0, blocking collectives: 4.93 us -> none  [stacked_from(): parts = lax.all_gather(parts, axes[k], axis=0, tiled=True)]
  transfers between devices with their start and end apart: 8 -> 7, of which waited for: 7 -> 6; matrix products, arithmetic and copies ran while one was open for 3% -> 3% of each run, Pallas kernels for 0% -> 0%
where the time goes in v1:
time: 447 us; the launch traced here: 446 us
  waiting for transfers between devices  303 us (68%)
  blocking collectives  48 us (11%)
  starting transfers between devices  44.7 us (10%)
  matrix products  18.7 us (4%)
  between operations  15.6 us (3%)
  other arithmetic  9.61 us (2%)
  local copies, waits for them, and re-layouts  6.22 us (1%)
    all_to_all x1, waiting for transfers between devices, per_device(): lax.all_to_all(text_store.astype(jnp.bfloat16), DP, split_axis=0, concat_...  163 us
    psum x1, waiting for transfers between devices, per_device(): image_out = image_float + lax.psum(partial_out, 'mp')  100 us
    all_to_all x2, waiting for transfers between devices, sum_at_owner(): lax.all_to_all(parts, axis, split_axis=0, concat_axis=0, tiled=True)  30.3 us
    all_to_all x1, blocking collectives, sent_to_all(): return lax.all_to_all(copies, axis, split_axis=0, concat_axis=0, tiled=True)  18.8 us
    all_to_all x1, blocking collectives, summed_on_arrival(): parts = lax.all_to_all(cut_along(array, dim, peers), axis, 0, 0, tiled=True)  16.3 us
    all_to_all x1, starting transfers between devices, stacked_from(): lax.all_to_all(jnp.stack([parts] * lax.axis_size(axes[k])), axes[k], 0, 0)  15 us
    all_to_all x1, starting transfers between devices, per_device(): lax.all_to_all(text_store.astype(jnp.bfloat16), DP, split_axis=0, concat_...  14.8 us
    all_to_all x2, blocking collectives, stacked_from(): lax.all_to_all(jnp.stack([parts] * lax.axis_size(axes[k])), axes[k], 0, 0)  12.9 us
  transfers between devices with their start and end apart: 7, of which 6 were waited for; matrix products, arithmetic and copies ran while one was open for 3% of the time, Pallas kernels for 0%

profile of v1, /device:TPU:8, one launch (start us, length us, event | category | flops | bytes accessed | tf_op | source)
XLA Modules:
  0.0 445.9 jit_solution(15980455903888004143)
XLA Ops:
  7.2 0.0 copy-start
  7.2 1.4 convolution_convert_fusion.1
  8.6 16.3 %all_to_all.55 = bf16[8,24,1152]{2,1,0:T(8,128)(2,1)S(1)} all-to-all(bf16[8,24,1152]{2,1,0:T(8,128)(2,1)S(1)} %bitcast.53), channel_id=1, replica_groups=mesh['dp_0'=16,'dp_1'=2,'dp_2'=2,'mp'=8] {'mp'}, dimensions={0} | all-to-all | bytes 884736 | tf_op jit(solution)/shard_map/all_to_all | solution.py:18
  24.9 0.1 convert_reduce_fusion.2
  25.0 0.0 copy-start.3
  25.0 0.1 multiply_reduce_fusion.3
  25.1 0.5 copy-done.3
  25.6 0.1 fusion.50
  25.7 6.4 %all_to_all.56 = bf16[2,1,24,1152]{3,2,1,0:T(8,128)(2,1)S(1)} all-to-all(bf16[2,1,24,1152]{3,2,1,0:T(8,128)(2,1)S(1)} %pad_maximum_fusion.1), channel_id=1, replica_groups=mesh['dp_0'=16,'dp_1'=2,'dp_2'=2,'mp'=8] {'dp_1'}, dimensions={0} | all-to-all | bytes 221184 | tf_op jit(solution)/shard_map/all_to_all | solution.py:32
  32.1 1.3 stack.10
  33.4 15.0 %all-to-all-start.2 = ((bf16[16,2,24,1152]{3,2,1,0:T(8,128)(2,1)}), bf16[16,2,24,1152]{3,2,1,0:T(8,128)(2,1)S(1)}, u32[]{:S(2)}, u32[]{:S(2)}) async-start(bf16[16,2,24,1152]{3,2,1,0:T(8,128)(2,1)} %stack.10), calls=%async_computation.2 | async-start | bytes 3538944 | tf_op jit(solution)/shard_map/all_to_all | solution.py:32
  48.5 0.0 all-reduce.2.cloned.1.call-start
  48.5 0.0 copy-done.1
  48.5 0.1 convert_reduce_fusion.1
  48.7 0.3 fusion.9
  49.0 0.0 copy-done.9
  49.0 2.0 fusion.22
  51.0 0.8 copy-done.7
  51.8 1.5 fusion.32
  53.3 0.0 all-reduce.2.cloned.1.call-update
  54.6 100.1 %all-reduce.2.cloned.1.call-done = f32[192,1152]{1,0:T(8,128)} async-done(((f32[192,1152]{1,0:T(8,128)}), f32[192,1152]{1,0:T(8,128)}) %all-reduce.2.cloned.1.call-update) | async-done | bytes 884752 | tf_op jit(solution)/shard_map/psum | solution.py:108
  154.7 1.5 multiply_reduce_fusion
  156.2 1.4 fusion.7
  157.5 0.0 all-to-all-done.2
  157.5 0.4 pad_maximum_fusion
  157.9 6.6 %all_to_all.57 = bf16[2,32,24,1152]{3,2,1,0:T(8,128)(2,1)S(1)} all-to-all(bf16[2,32,24,1152]{3,2,1,0:T(8,128)(2,1)S(1)} %pad_maximum_fusion), channel_id=1, replica_groups=mesh['dp_0'=16,'dp_1'=2,'dp_2'=2,'mp'=8] {'dp_2'}, dimensions={0} | all-to-all | bytes 7077888 | tf_op jit(solution)/shard_map/all_to_all | solution.py:32
  164.5 0.3 copy.21
  164.8 0.7 copy-done.6
  165.5 2.5 fusion.6
  168.0 1.9 fusion.74
  169.9 3.5 all-to-all-start.4
  173.4 0.1 dynamic-slice.3
  173.5 14.7 %all-to-all-done.4 = f32[8,24,1152]{2,1,0:T(8,128)S(1)} async-done(((f32[8,24,1152]{2,1,0:T(8,128)}), f32[8,24,1152]{2,1,0:T(8,128)S(1)}, u32[]{:S(2)}, u32[]{:S(2)}) %all-to-all-start.4) | async-done | bytes 884768 | tf_op jit(solution)/shard_map/all_to_all | solution.py:46
  188.2 0.1 fusion.43
  188.4 0.1 fusion.45
  188.5 0.0 copy-start.8
  188.5 0.1 broadcast_in_dim.35
  188.5 18.8 %all_to_all.58 = f32[8,24,1152]{2,1,0:T(8,128)S(1)} all-to-all(f32[8,24,1152]{2,1,0:T(8,128)S(1)} %broadcast_in_dim.35), channel_id=1, replica_groups=mesh['dp_0'=16,'dp_1'=2,'dp_2'=2,'mp'=8] {'mp'}, dimensions={0} | all-to-all | bytes 1769472 | tf_op jit(solution)/shard_map/all_to_all | solution.py:52
  207.3 3.7 fusion.28
  211.0 3.6 all-to-all-start.6
  214.6 0.1 dynamic_slice.15
  214.7 15.6 %all-to-all-done.6 = f32[8,192,144]{1,2,0:T(8,128)S(1)} async-done(((f32[8,192,144]{1,2,0:T(8,128)}), f32[8,192,144]{1,2,0:T(8,128)S(1)}, u32[]{:S(2)}, u32[]{:S(2)}) %all-to-all-start.6) | async-done | bytes 884768 | tf_op jit(solution)/shard_map/all_to_all | solution.py:46
  230.3 0.1 reduce_sum.127
  230.4 0.1 copy.23
  230.5 1.2 multiply_reduce_fusion.2
  231.7 0.1 pad_maximum_fusion.2
  231.8 0.6 broadcast_in_dim.36
  232.4 3.8 all-to-all-start.7
  236.2 4.8 %convolution_convert_fusion = bf16[1536,1152]{1,0:T(8,128)(2,1)} fusion(bf16[192,1152]{1,0:T(8,128)(2,1)} %get-tuple-element.15, f32[1536,192]{0,1:T(8,128)} %get-tuple-element.19, s32[1536]{0:T(1024)S(1)} %fusion.59, f32[]{:T(128)S(6)} %copy.31, s32[192]{0:T(256)S(1)} %iota_add_fusion), kind=kOutput, calls=%fused_computation | convolution fusion | flops 684195840 | bytes 5167876 | tf_op jit(solution)/shard_map/dot_general | solution.py:141
  241.0 2.9 all-to-all-done.7
  243.9 14.8 %all-to-all-start.8 = ((bf16[64,24,1152]{2,1,0:T(8,128)(2,1)}), bf16[64,24,1152]{2,1,0:T(8,128)(2,1)}, u32[]{:S(2)}, u32[]{:S(2)}) async-start(bf16[64,24,1152]{2,1,0:T(8,128)(2,1)} %bitcast.51), calls=%async_computation.8 | async-start | bytes 7077888 | tf_op jit(solution)/shard_map/all_to_all | solution.py:145
  258.7 0.0 copy-start.4
  258.7 162.7 %all-to-all-done.8 = bf16[64,24,1152]{2,1,0:T(8,128)(2,1)} async-done(((bf16[64,24,1152]{2,1,0:T(8,128)(2,1)}), bf16[64,24,1152]{2,1,0:T(8,128)(2,1)}, u32[]{:S(2)}, u32[]{:S(2)}) %all-to-all-start.8) | async-done | bytes 3538976 | tf_op jit(solution)/shard_map/all_to_all | solution.py:145
  421.4 2.5 convert_reduce_fusion
  423.9 0.2 fusion.46
  424.1 0.1 fusion.49
  424.2 0.0 copy-start.5
  424.2 0.8 broadcast_in_dim.39
  425.0 3.9 all-to-all-start.9
  428.9 0.1 slice_multiply_fusion.1
  429.0 1.2 multiply_add_fusion
  430.2 0.8 copy.25
  430.9 7.1 %all-to-all-done.9 = bf16[8,24,1152]{2,1,0:T(8,128)(2,1)S(1)} async-done(((bf16[8,24,1152]{2,1,0:T(8,128)(2,1)}), bf16[8,24,1152]{2,1,0:T(8,128)(2,1)S(1)}, u32[]{:S(2)}, u32[]{:S(2)}) %all-to-all-start.9) | async-done | bytes 442400 | tf_op jit(solution)/shard_map/all_to_all | solution.py:52
  438.1 1.0 fusion.75
  (19 shorter events, 0.2 us)
Async XLA Ops:
  7.2 44.6 %copy-start = (bf16[538,1152]{1,0:T(8,128)(2,1)S(1)}, bf16[538,1152]{1,0:T(8,128)(2,1)}, u32[]{:S(2)}) copy-start(bf16[538,1152]{1,0:T(8,128)(2,1)} %param.12) | copy-start | bytes 3718660
  25.0 0.6 copy-start.3
  33.4 15.1 %copy-start.1 = (bf16[192,1152]{1,0:T(8,128)(2,1)S(1)}, bf16[192,1152]{1,0:T(8,128)(2,1)}, u32[]{:S(2)}) copy-start(bf16[192,1152]{1,0:T(8,128)(2,1)} %param.8) | copy-start | bytes 1327108
  33.4 15.5 %copy-start.9 = (f32[1152]{0:T(1024)S(1)}, f32[1152]{0:T(1024)}, u32[]{:S(2)}) copy-start(f32[1152]{0:T(1024)} %param.10) | copy-start | bytes 13828
  33.4 124.1 %all-to-all-start.2 = ((bf16[16,2,24,1152]{3,2,1,0:T(8,128)(2,1)}), bf16[16,2,24,1152]{3,2,1,0:T(8,128)(2,1)S(1)}, u32[]{:S(2)}, u32[]{:S(2)}) async-start(bf16[16,2,24,1152]{3,2,1,0:T(8,128)(2,1)} %stack.10), calls=%async_computation.2 | async-start | bytes 3538944 | tf_op jit(solution)/shard_map/all_to_all | solution.py:32
  48.5 106.2 %all-reduce.2.cloned.1.call-start = ((), (), s32[]{:S(2)}) async-start(), calls=%async_computation.10 | async-start | bytes 1769472 | tf_op jit(solution)/shard_map/psum | solution.py:108
  51.0 0.8 copy-start.7
  154.7 1.5 copy-start.2
  164.5 1.0 copy-start.6
  169.9 18.3 %all-to-all-start.4 = ((f32[8,24,1152]{2,1,0:T(8,128)}), f32[8,24,1152]{2,1,0:T(8,128)S(1)}, u32[]{:S(2)}, u32[]{:S(2)}) async-start(f32[8,24,1152]{2,1,0:T(8,128)} %fusion.74), calls=%async_computation.4 | async-start | bytes 1769472 | tf_op jit(solution)/shard_map/all_to_all | solution.py:46
  188.5 18.9 %copy-start.8 = (f32[192,538]{1,0:T(8,128)S(1)}, f32[192,538]{1,0:T(8,128)}, u32[]{:S(2)}) copy-start(f32[192,538]{1,0:T(8,128)} %copy-done.7) | copy-start | bytes 1239556
  211.0 19.2 %all-to-all-start.6 = ((f32[8,192,144]{1,2,0:T(8,128)}), f32[8,192,144]{1,2,0:T(8,128)S(1)}, u32[]{:S(2)}, u32[]{:S(2)}) async-start(f32[8,192,144]{1,2,0:T(8,128)} %bitcast.56), calls=%async_computation.6 | async-start | bytes 2359296 | tf_op jit(solution)/shard_map/all_to_all | solution.py:46
  232.4 11.5 %all-to-all-start.7 = ((f32[8,1,384]{2,1,0:T(1,128)}), f32[8,1,384]{2,1,0:T(1,128)S(1)}, u32[]{:S(2)}, u32[]{:S(2)}) async-start(f32[8,1,384]{2,1,0:T(1,128)} %broadcast_in_dim.36), calls=%async_computation.7 | async-start | bytes 24576 | tf_op jit(solution)/shard_map/all_to_all | solution.py:52
  243.9 177.5 %all-to-all-start.8 = ((bf16[64,24,1152]{2,1,0:T(8,128)(2,1)}), bf16[64,24,1152]{2,1,0:T(8,128)(2,1)}, u32[]{:S(2)}, u32[]{:S(2)}) async-start(bf16[64,24,1152]{2,1,0:T(8,128)(2,1)} %bitcast.51), calls=%async_computation.8 | async-start | bytes 7077888 | tf_op jit(solution)/shard_map/all_to_all | solution.py:145
  258.7 165.2 %copy-start.4 = (f32[24,1152]{1,0:T(8,128)S(1)}, f32[24,1152]{1,0:T(8,128)}, u32[]{:S(2)}) copy-start(f32[24,1152]{1,0:T(8,128)} %copy-done.3) | copy-start | bytes 331780
  424.2 13.9 %copy-start.5 = (bf16[144,1152]{1,0:T(8,128)(2,1)S(1)}, bf16[144,1152]{1,0:T(8,128)(2,1)}, u32[]{:S(2)}) copy-start(bf16[144,1152]{1,0:T(8,128)(2,1)} %param.13) | copy-start | bytes 995332
  425.0 13.0 %all-to-all-start.9 = ((bf16[8,24,1152]{2,1,0:T(8,128)(2,1)}), bf16[8,24,1152]{2,1,0:T(8,128)(2,1)S(1)}, u32[]{:S(2)}, u32[]{:S(2)}) async-start(bf16[8,24,1152]{2,1,0:T(8,128)(2,1)} %broadcast_in_dim.39), calls=%async_computation.9 | async-start | bytes 884736 | tf_op jit(solution)/shard_map/all_to_all | solution.py:52
Sparse Core Ops, SparseCore 0:
  53.4 101.2 all-reduce.1
